TPU v7x, 32 devices: a whole 2x2x4 slice. The times are simulated.
32 devices in a mesh: depth: 4 (over y, x), screen: 8 (over z, core).
Axes of the slice: x: 2, y: 2, z: 4, core: 2. Of those that a mesh axis runs over, the one named last changes fastest.
Arguments:
- voxel_bins: int32 [32, 256, 2048], P('depth', None, 'screen'), may hold values from 0 to 255
- colors: bfloat16 [3, 256], replicated, may hold values from 0 to 2
- opacity: bfloat16 [256], replicated, may hold values from 0 to 1
- slab_order: int32 [8, 4], replicated, may hold values from 0 to 3, each once within a row
Outputs:
- image: float32 [4, 256, 2048], P(None, ('depth', 'screen'))
Inputs may be any that keep to these rules, and one draw needn't show every extreme that they name: `slab_order`: every row is a permutation of 0 to 3.
All inputs are finite; a program needn't handle non-finite values.
Results may differ from a plain program's by a relative error of at most 0.0003.
Values sent between devices are 32-bit elements; how exact they have to be, the bound alone decides.
No kernel may reach another device: no remote copies, remote signals or barrier semaphores. Data moves between devices by JAX's collectives and lax.ppermute only.
A program may use at most 64 MiB of HBM per device.

v0:
```python
import math
import jax
import jax.numpy as jnp
from jax import lax
from jax.sharding import PartitionSpec as P

low_count = 16
extinction = 3.0


def look_up(table_rows, bin_block):
    high_count = table_rows.shape[0] // 4
    low_part = bin_block % low_count
    high_part = bin_block // low_count
    low_onehot = (low_part[None, :] == jnp.arange(low_count, dtype=jnp.int32)[:, None]).astype(
        jnp.bfloat16
    )
    picked = jnp.dot(table_rows, low_onehot, preferred_element_type=jnp.float32)
    picked = picked.reshape(4, high_count, bin_block.shape[0])
    high_match = high_part[None, :] == jnp.arange(high_count, dtype=jnp.int32)[:, None]
    return jnp.sum(jnp.where(high_match[None], picked, 0.0), axis=1)


def render(voxel_bins, table_rows, total_samples):
    samples_here, row_count, col_count = voxel_bins.shape
    pixels = row_count * col_count
    per_step = math.gcd(samples_here, max(1, 131072 // pixels))
    blocks = voxel_bins.reshape(samples_here // per_step, per_step * pixels)
    extinct_rate = extinction / total_samples

    def advance(carried, bin_block):
        passed, color_sum = carried
        values = look_up(table_rows, bin_block).reshape(4, per_step, pixels)
        density = values[3]
        before = jnp.cumsum(density, axis=0) - density
        weight = (1.0 - jnp.exp(-extinct_rate * density)) * jnp.exp(
            -extinct_rate * (passed[None] + before)
        )
        color_sum = color_sum + jnp.sum(weight[None] * values[:3], axis=1)
        return ((passed + jnp.sum(density, axis=0), color_sum), None)

    start = (jnp.zeros((pixels,), jnp.float32), jnp.zeros((3, pixels), jnp.float32))
    (passed, color_sum), ignored = lax.scan(advance, start, blocks)
    final_alpha = 1.0 - jnp.exp(-extinct_rate * passed)
    partial_value = jnp.concatenate([color_sum, final_alpha[None]], axis=0)
    return partial_value.reshape(4, row_count, col_count)


def composite(pieces, places):
    in_front = (places[:, None, :] < places[:, :, None]).astype(jnp.float32)
    clear_log = jnp.log1p(-pieces[:, :, 3])
    front_log = jnp.einsum("tij,jtrw->itrw", in_front, clear_log, precision=lax.Precision.HIGHEST)
    shaded = jnp.sum(pieces[:, :, :3] * jnp.exp(front_log)[:, :, None], axis=0)
    total_alpha = 1.0 - jnp.exp(jnp.sum(clear_log, axis=0))
    merged = jnp.concatenate([shaded, total_alpha[:, None]], axis=1)
    return jnp.transpose(merged, (1, 2, 0, 3))


def local(voxel_bins, colors, opacity, slab_order):
    table = jnp.concatenate([colors, opacity[None]], axis=0)
    table_rows = table.reshape(4 * (table.shape[1] // low_count), low_count)
    depth_count = lax.axis_size("depth")
    total_samples = voxel_bins.shape[0] * depth_count
    partial_value = render(voxel_bins, table_rows, total_samples)
    own_order = lax.dynamic_slice_in_dim(slab_order, lax.axis_index("screen"), 1, 0)
    tile_block = composite(
        lax.all_to_all(partial_value[None], "depth", split_axis=2, concat_axis=0, tiled=True)[
            :, None
        ],
        own_order,
    )[:, :, 0]
    result = lax.all_to_all(tile_block, "screen", split_axis=1, concat_axis=2, tiled=True)
    return result


def solution(mesh):
    placed = (P("depth", None, "screen"), P(), P(), P())
    return jax.shard_map(
        local,
        mesh=mesh,
        in_specs=placed,
        out_specs=P(None, ("depth", "screen"), None),
        check_vma=False,
    )
```

profile of v0, /device:TPU:0, one launch (start us, length us, event | category | flops | bytes accessed | tf_op | source)
XLA Modules:
  0.0 185.4 jit_solution(1392531687887182417)
XLA Ops:
  0.0 4.0 %reshape.163 = s32[4,131072]{1,0:T(4,128)} reshape(s32[8,256,256]{2,1,0:T(8,128)} %param.6) | data formatting | bytes 4194304 | tf_op jit(solution)/shard_map/reshape | solution.py:28
  4.2 141.1 %while.15 = (s32[]{:T(128)}, f32[65536]{0:T(1024)}, f32[3,65536]{1,0:T(4,128)}, s32[4,131072]{1,0:T(4,128)}, bf16[64,16]{0,1:T(8,128)(2,1)S(1)}, /*index=5*/s32[]{:T(128)}, f32[]{:T(128)}, s32[]{:T(128)}) while((s32[]{:T(128)}, f32[65536]{0:T(1024)}, f32[3,65536]{1,0:T(4,128)}, s32[4,131072]{1,0:T(4,128)}, ...), condition=%wide.region_5.6_spmd.clone, body=%wide.region_0.5_spmd.clone.sunk | while | flops 293994496 | bytes 31983784 | solution.py:43
  4.2 3.4 %and_select_fusion.4 = (s32[1,131072]{1,0:T(1,128)S(1)}, s32[1,131072]{1,0:T(1,128)S(1)}) fusion(s32[4,131072]{1,0:T(4,128)} %get-tuple-element.186, s32[]{:T(128)} %get-tuple-element.175), kind=kLoop, calls=%fused_computation.5.clone.1 | loop fusion | flops 1441792 | bytes 1572868 | tf_op jit(solution)/shard_map/while/body/eval_jaxpr/jit(remainder)/select_n | solution.py:13
  7.6 3.8 %and_select_fusion.5 = s32[1,131072]{1,0:T(1,128)S(1)} fusion(s32[1,131072]{1,0:T(1,128)S(1)} %get-tuple-element.163, s32[4,131072]{1,0:T(4,128)} %get-tuple-element.186, s32[]{:T(128)} %get-tuple-element.175), kind=kLoop, calls=%fused_computation.6.clone.1 | loop fusion | flops 1572864 | bytes 1572868 | tf_op jit(solution)/shard_map/while/body/eval_jaxpr/jit(floor_divide)/jit(_where)/select_n | solution.py:14
  12.5 11.0 %select_reduce_fusion.2 = f32[4,131072]{1,0:T(4,128)S(1)} fusion(pred[16,131072]{1,0:T(8,128)(4,1)S(1)} %iota_compare_fusion.4, bf16[64,16]{0,1:T(8,128)(2,1)S(1)} %get-tuple-element.187, s32[131072]{0:T(1024)S(1)} %bitcast.47), kind=kOutput, calls=%fused_computation.clone.1 | convolution fusion | flops 286785536 | bytes 4720640 | tf_op jit(solution)/shard_map/while/body/eval_jaxpr/dot_general | solution.py:18
  30.5 2.9 %slice.46 = f32[3,2,65536]{2,1,0:T(2,128)} reshape(f32[3,131072]{1,0:T(4,128)S(1)} %bitcast.45) | data formatting | bytes 3145728 | tf_op jit(solution)/shard_map/while/body/eval_jaxpr/slice | solution.py:39
  33.3 3.9 %multiply_reduce_fusion.2 = f32[3,65536]{1,0:T(4,128)S(1)} fusion(f32[3,2,65536]{2,1,0:T(2,128)} %slice.46, f32[2,65536]{1,0:T(2,128)S(1)} %exponential_multiply_fusion.2), kind=kLoop, calls=%fused_computation.7.clone.1 | loop fusion | flops 589824 | bytes 2883584 | tf_op jit(solution)/shard_map/while/body/eval_jaxpr/reduce_sum | solution.py:39
  38.8 3.4 %and_select_fusion.4 = (s32[1,131072]{1,0:T(1,128)S(1)}, s32[1,131072]{1,0:T(1,128)S(1)}) fusion(s32[4,131072]{1,0:T(4,128)} %get-tuple-element.186, s32[]{:T(128)} %get-tuple-element.175), kind=kLoop, calls=%fused_computation.5.clone.1 | loop fusion | flops 1441792 | bytes 1572868 | tf_op jit(solution)/shard_map/while/body/eval_jaxpr/jit(remainder)/select_n | solution.py:13
  42.2 3.8 %and_select_fusion.5 = s32[1,131072]{1,0:T(1,128)S(1)} fusion(s32[1,131072]{1,0:T(1,128)S(1)} %get-tuple-element.163, s32[4,131072]{1,0:T(4,128)} %get-tuple-element.186, s32[]{:T(128)} %get-tuple-element.175), kind=kLoop, calls=%fused_computation.6.clone.1 | loop fusion | flops 1572864 | bytes 1572868 | tf_op jit(solution)/shard_map/while/body/eval_jaxpr/jit(floor_divide)/jit(_where)/select_n | solution.py:14
  47.0 11.0 %select_reduce_fusion.2 = f32[4,131072]{1,0:T(4,128)S(1)} fusion(pred[16,131072]{1,0:T(8,128)(4,1)S(1)} %iota_compare_fusion.4, bf16[64,16]{0,1:T(8,128)(2,1)S(1)} %get-tuple-element.187, s32[131072]{0:T(1024)S(1)} %bitcast.47), kind=kOutput, calls=%fused_computation.clone.1 | convolution fusion | flops 286785536 | bytes 4720640 | tf_op jit(solution)/shard_map/while/body/eval_jaxpr/dot_general | solution.py:18
  66.0 2.9 %slice.46 = f32[3,2,65536]{2,1,0:T(2,128)} reshape(f32[3,131072]{1,0:T(4,128)S(1)} %bitcast.45) | data formatting | bytes 3145728 | tf_op jit(solution)/shard_map/while/body/eval_jaxpr/slice | solution.py:39
  68.8 3.9 %multiply_reduce_fusion.2 = f32[3,65536]{1,0:T(4,128)S(1)} fusion(f32[3,2,65536]{2,1,0:T(2,128)} %slice.46, f32[2,65536]{1,0:T(2,128)S(1)} %exponential_multiply_fusion.2), kind=kLoop, calls=%fused_computation.7.clone.1 | loop fusion | flops 589824 | bytes 2883584 | tf_op jit(solution)/shard_map/while/body/eval_jaxpr/reduce_sum | solution.py:39
  74.3 3.4 %and_select_fusion.4 = (s32[1,131072]{1,0:T(1,128)S(1)}, s32[1,131072]{1,0:T(1,128)S(1)}) fusion(s32[4,131072]{1,0:T(4,128)} %get-tuple-element.186, s32[]{:T(128)} %get-tuple-element.175), kind=kLoop, calls=%fused_computation.5.clone.1 | loop fusion | flops 1441792 | bytes 1572868 | tf_op jit(solution)/shard_map/while/body/eval_jaxpr/jit(remainder)/select_n | solution.py:13
  77.7 3.8 %and_select_fusion.5 = s32[1,131072]{1,0:T(1,128)S(1)} fusion(s32[1,131072]{1,0:T(1,128)S(1)} %get-tuple-element.163, s32[4,131072]{1,0:T(4,128)} %get-tuple-element.186, s32[]{:T(128)} %get-tuple-element.175), kind=kLoop, calls=%fused_computation.6.clone.1 | loop fusion | flops 1572864 | bytes 1572868 | tf_op jit(solution)/shard_map/while/body/eval_jaxpr/jit(floor_divide)/jit(_where)/select_n | solution.py:14
  82.5 11.0 %select_reduce_fusion.2 = f32[4,131072]{1,0:T(4,128)S(1)} fusion(pred[16,131072]{1,0:T(8,128)(4,1)S(1)} %iota_compare_fusion.4, bf16[64,16]{0,1:T(8,128)(2,1)S(1)} %get-tuple-element.187, s32[131072]{0:T(1024)S(1)} %bitcast.47), kind=kOutput, calls=%fused_computation.clone.1 | convolution fusion | flops 286785536 | bytes 4720640 | tf_op jit(solution)/shard_map/while/body/eval_jaxpr/dot_general | solution.py:18
  101.5 2.9 %slice.46 = f32[3,2,65536]{2,1,0:T(2,128)} reshape(f32[3,131072]{1,0:T(4,128)S(1)} %bitcast.45) | data formatting | bytes 3145728 | tf_op jit(solution)/shard_map/while/body/eval_jaxpr/slice | solution.py:39
  104.3 3.9 %multiply_reduce_fusion.2 = f32[3,65536]{1,0:T(4,128)S(1)} fusion(f32[3,2,65536]{2,1,0:T(2,128)} %slice.46, f32[2,65536]{1,0:T(2,128)S(1)} %exponential_multiply_fusion.2), kind=kLoop, calls=%fused_computation.7.clone.1 | loop fusion | flops 589824 | bytes 2883584 | tf_op jit(solution)/shard_map/while/body/eval_jaxpr/reduce_sum | solution.py:39
  109.8 3.4 %and_select_fusion.4 = (s32[1,131072]{1,0:T(1,128)S(1)}, s32[1,131072]{1,0:T(1,128)S(1)}) fusion(s32[4,131072]{1,0:T(4,128)} %get-tuple-element.186, s32[]{:T(128)} %get-tuple-element.175), kind=kLoop, calls=%fused_computation.5.clone.1 | loop fusion | flops 1441792 | bytes 1572868 | tf_op jit(solution)/shard_map/while/body/eval_jaxpr/jit(remainder)/select_n | solution.py:13
  113.2 3.8 %and_select_fusion.5 = s32[1,131072]{1,0:T(1,128)S(1)} fusion(s32[1,131072]{1,0:T(1,128)S(1)} %get-tuple-element.163, s32[4,131072]{1,0:T(4,128)} %get-tuple-element.186, s32[]{:T(128)} %get-tuple-element.175), kind=kLoop, calls=%fused_computation.6.clone.1 | loop fusion | flops 1572864 | bytes 1572868 | tf_op jit(solution)/shard_map/while/body/eval_jaxpr/jit(floor_divide)/jit(_where)/select_n | solution.py:14
  118.0 11.0 %select_reduce_fusion.2 = f32[4,131072]{1,0:T(4,128)S(1)} fusion(pred[16,131072]{1,0:T(8,128)(4,1)S(1)} %iota_compare_fusion.4, bf16[64,16]{0,1:T(8,128)(2,1)S(1)} %get-tuple-element.187, s32[131072]{0:T(1024)S(1)} %bitcast.47), kind=kOutput, calls=%fused_computation.clone.1 | convolution fusion | flops 286785536 | bytes 4720640 | tf_op jit(solution)/shard_map/while/body/eval_jaxpr/dot_general | solution.py:18
  139.8 3.9 %multiply_reduce_fusion.2 = f32[3,65536]{1,0:T(4,128)S(1)} fusion(f32[3,2,65536]{2,1,0:T(2,128)} %slice.46, f32[2,65536]{1,0:T(2,128)S(1)} %exponential_multiply_fusion.2), kind=kLoop, calls=%fused_computation.7.clone.1 | loop fusion | flops 589824 | bytes 2883584 | tf_op jit(solution)/shard_map/while/body/eval_jaxpr/reduce_sum | solution.py:39
  149.0 5.2 %all-to-all-start = ((f32[1,4,256,256]{3,1,0,2:T(4,128)}), f32[1,4,256,256]{3,1,0,2:T(4,128)S(1)}, u32[]{:S(2)}, u32[]{:S(2)}) async-start(f32[1,4,256,256]{3,1,0,2:T(4,128)} %pad_maximum_fusion), calls=%async_computation | async-start | bytes 2097152 | tf_op jit(solution)/shard_map/all_to_all | solution.py:67
  154.4 13.4 %all-to-all-done = f32[1,4,256,256]{3,1,0,2:T(4,128)S(1)} async-done(((f32[1,4,256,256]{3,1,0,2:T(4,128)}), f32[1,4,256,256]{3,1,0,2:T(4,128)S(1)}, u32[]{:S(2)}, u32[]{:S(2)}) %all-to-all-start) | async-done | bytes 1048608 | tf_op jit(solution)/shard_map/all_to_all | solution.py:67
  170.2 14.4 %all_to_all.33 = f32[4,64,256]{2,0,1:T(4,128)S(1)} all-to-all(f32[4,64,256]{2,0,1:T(4,128)S(1)} %copy.19), channel_id=1, replica_groups=mesh['depth'=4,'screen'=8] {'screen'}, dimensions={1} | all-to-all | bytes 524288 | tf_op jit(solution)/shard_map/all_to_all | solution.py:72
  (72 shorter events, 51.1 us)
Async XLA Ops:
  0.0 154.2 %copy-start = (s32[8,4]{0,1:T(4,128)S(1)}, s32[8,4]{0,1:T(4,128)}, u32[]{:S(2)}) copy-start(s32[8,4]{0,1:T(4,128)} %param.9) | copy-start | bytes 388
  0.0 4.0 %copy-start.4 = (bf16[256]{0:T(256)(128)(2,1)S(1)}, bf16[256]{0:T(256)(128)(2,1)}, u32[]{:S(2)}) copy-start(bf16[256]{0:T(256)(128)(2,1)} %param.8) | copy-start | bytes 1540
  0.0 4.0 %copy-start.3 = (bf16[3,256]{1,0:T(4,128)(2,1)S(1)}, bf16[3,256]{1,0:T(4,128)(2,1)}, u32[]{:S(2)}) copy-start(bf16[3,256]{1,0:T(4,128)(2,1)} %param.7) | copy-start | bytes 4612
  33.3 3.9 %copy-start.1 = (f32[3,65536]{1,0:T(4,128)S(1)}, f32[3,65536]{1,0:T(4,128)}, u32[]{:S(2)}) copy-start(f32[3,65536]{1,0:T(4,128)} %get-tuple-element.177) | copy-start | bytes 2359300 | tf_op jit(solution)/shard_map/while
  37.8 1.0 copy-start.2
  68.8 3.9 %copy-start.1 = (f32[3,65536]{1,0:T(4,128)S(1)}, f32[3,65536]{1,0:T(4,128)}, u32[]{:S(2)}) copy-start(f32[3,65536]{1,0:T(4,128)} %get-tuple-element.177) | copy-start | bytes 2359300 | tf_op jit(solution)/shard_map/while
  73.4 1.0 copy-start.2
  104.3 3.9 %copy-start.1 = (f32[3,65536]{1,0:T(4,128)S(1)}, f32[3,65536]{1,0:T(4,128)}, u32[]{:S(2)}) copy-start(f32[3,65536]{1,0:T(4,128)} %get-tuple-element.177) | copy-start | bytes 2359300 | tf_op jit(solution)/shard_map/while
  108.9 1.0 copy-start.2
  139.8 3.9 %copy-start.1 = (f32[3,65536]{1,0:T(4,128)S(1)}, f32[3,65536]{1,0:T(4,128)}, u32[]{:S(2)}) copy-start(f32[3,65536]{1,0:T(4,128)} %get-tuple-element.177) | copy-start | bytes 2359300 | tf_op jit(solution)/shard_map/while
  144.4 1.0 copy-start.2
  149.0 18.8 %all-to-all-start = ((f32[1,4,256,256]{3,1,0,2:T(4,128)}), f32[1,4,256,256]{3,1,0,2:T(4,128)S(1)}, u32[]{:S(2)}, u32[]{:S(2)}) async-start(f32[1,4,256,256]{3,1,0,2:T(4,128)} %pad_maximum_fusion), calls=%async_computation | async-start | bytes 2097152 | tf_op jit(solution)/shard_map/all_to_all | solution.py:67
where the time goes:
time: 186 us; the launch traced here: 185 us
  other arithmetic  78.4 us (42%)
  matrix products  44.8 us (24%)
  local copies, waits for them, and re-layouts  28.7 us (15%)
  blocking collectives  14.4 us (8%)
  waiting for transfers between devices  13.4 us (7%)
  starting transfers between devices  5.19 us (3%)
    dot_general x4, matrix products, look_up(): picked = jnp.dot(table_rows, low_onehot, preferred_element_type=jnp.float32)  44.2 us
    reduce_sum x4, other arithmetic, advance(): color_sum = color_sum + jnp.sum(weight[None] * values[:3], axis=1)  15.5 us
    select_n x4, other arithmetic, look_up(): high_part = bin_block // low_count  15 us
    all_to_all x1, blocking collectives, local(): lax.all_to_all(tile_block, 'screen', split_axis=1, concat_axis=2, tiled=T...  14.4 us
    select_n x4, other arithmetic, look_up(): low_part = bin_block % low_count  13.5 us
    all_to_all x1, waiting for transfers between devices, local(): lax.all_to_all(partial_value[None], 'depth', split_axis=2, concat_axis=0,...  13.4 us
    slice x4, local copies, waits for them, and re-layouts, advance(): color_sum = color_sum + jnp.sum(weight[None] * values[:3], axis=1)  11.4 us
    another operation x4, other arithmetic, advance(): before = jnp.cumsum(density, axis=0) - density  7.29 us
  transfers between devices with their start and end apart: 1, of which 1 were waited for; matrix products, arithmetic and copies ran while one was open for 0% of the time, Pallas kernels for 0%

commit v1 on v0

--- a/solution.py
+++ b/solution.py
@@ -6,6 +6,18 @@
 
 low_count = 16
 extinction = 3.0
+
+
+def in_blocks(value, dim, length):
+    shape = value.shape
+    blocks = value.reshape(*shape[:dim], length, shape[dim] // length, *shape[dim + 1 :])
+    return jnp.moveaxis(blocks, dim, 0)
+
+
+def joined_along(tiles, dim):
+    tiles = jnp.moveaxis(tiles, 0, dim)
+    shape = tiles.shape
+    return tiles.reshape(*shape[:dim], shape[dim] * shape[dim + 1], *shape[dim + 2 :])
 
 
 def look_up(table_rows, bin_block):
@@ -69,7 +81,15 @@
         ],
         own_order,
     )[:, :, 0]
-    result = lax.all_to_all(tile_block, "screen", split_axis=1, concat_axis=2, tiled=True)
+    peers, index = (lax.axis_size("screen"), lax.axis_index("screen"))
+    parts = in_blocks(tile_block, 1, peers)
+    out = parts
+    for step in range(1, peers):
+        target, source = ((index + step) % peers, (index - step) % peers)
+        sent = lax.dynamic_index_in_dim(parts, target, 0)
+        other = lax.ppermute(sent, "screen", [(i, (i + step) % peers) for i in range(peers)])
+        out = lax.dynamic_update_slice_in_dim(out, other, source, axis=0)
+    result = joined_along(out, 2)
     return result
 
 

time: 186 us -> 150 us (0.81)
  other arithmetic: 78.4 us -> 47.5 us
  blocking collectives: 14.4 us -> 0 us
  starting transfers between devices: 5.19 us -> 14.7 us
    all_to_all x1 -> x0, blocking collectives: 14.4 us -> none  [local(): lax.all_to_all(tile_block, 'screen', split_axis=1, concat_axis=2, tiled=T...]
    ppermute x0 -> x7, starting transfers between devices: none -> 9.49 us  [local(): lax.ppermute(sent, 'screen', [(i, (i + step) % peers) for i in range(peer...]
    select_n x4, other arithmetic: 13.5 us -> 7.1 us  [look_up(): low_part = bin_block % low_count]
    select_n x4, other arithmetic: 15 us -> 8.8 us  [look_up(): high_part = bin_block // low_count]
    add x4, other arithmetic: 5.98 us -> 0.28 us  [advance(): return ((passed + jnp.sum(density, axis=0), color_sum), None)]
    mul x4, other arithmetic: 7.29 us -> 2.88 us  [advance(): (1.0 - jnp.exp(-extinct_rate * density)) * jnp.exp(-extinct_rate * (passe...]
    reduce_sum x4, other arithmetic: 15.5 us -> 11.2 us  [advance(): color_sum = color_sum + jnp.sum(weight[None] * values[:3], axis=1)]
    another operation x4, other arithmetic: 7.29 us -> 4.24 us  [advance(): before = jnp.cumsum(density, axis=0) - density]
  transfers between devices with their start and end apart: 1 -> 8, of which waited for: 1 -> 3; matrix products, arithmetic and copies ran while one was open for 0% -> 0% of each run, Pallas kernels for 0% -> 0%
where the time goes in v1:
time: 150 us
  other arithmetic  47.5 us (32%)
  matrix products  44.8 us (30%)
  local copies, waits for them, and re-layouts  27.3 us (18%)
  waiting for transfers between devices  14.9 us (10%)
  starting transfers between devices  14.7 us (10%)
    dot_general x4, matrix products, look_up(): picked = jnp.dot(table_rows, low_onehot, preferred_element_type=jnp.float32)  44.2 us
    all_to_all x1, waiting for transfers between devices, local(): lax.all_to_all(partial_value[None], 'depth', split_axis=2, concat_axis=0,...  13.4 us
    slice x4, local copies, waits for them, and re-layouts, advance(): color_sum = color_sum + jnp.sum(weight[None] * values[:3], axis=1)  11.4 us
    reduce_sum x4, other arithmetic, advance(): color_sum = color_sum + jnp.sum(weight[None] * values[:3], axis=1)  11.2 us
    ppermute x7, starting transfers between devices, local(): lax.ppermute(sent, 'screen', [(i, (i + step) % peers) for i in range(peer...  9.49 us
    select_n x4, other arithmetic, look_up(): high_part = bin_block // low_count  8.8 us
    select_n x4, other arithmetic, look_up(): low_part = bin_block % low_count  7.1 us
    slice x4, local copies, waits for them, and re-layouts, advance(): density = values[3]  6.27 us
  transfers between devices with their start and end apart: 8, of which 3 were waited for; matrix products, arithmetic and copies ran while one was open for 0% of the time, Pallas kernels for 0%

profile of v1, /device:TPU:0, one launch (start us, length us, event | category | flops | bytes accessed | tf_op | source)
XLA Modules:
  0.0 149.8 jit_solution(13506434463822965748)
XLA Ops:
  0.0 2.7 %reshape.180 = s32[4,131072]{1,0:T(4,128)S(1)} reshape(s32[8,256,256]{2,1,0:T(8,128)} %param.6) | data formatting | bytes 4194304 | tf_op jit(solution)/shard_map/reshape | solution.py:40
  2.9 111.3 %while.15 = (s32[]{:T(128)}, f32[65536]{0:T(1024)S(1)}, f32[3,65536]{1,0:T(4,128)}, s32[4,131072]{1,0:T(4,128)S(1)}, bf16[64,16]{0,1:T(8,128)(2,1)S(1)}, /*index=5*/s32[]{:T(128)}, f32[]{:T(128)}, s32[]{:T(128)}) while((s32[]{:T(128)}, f32[65536]{0:T(1024)S(1)}, f32[3,65536]{1,0:T(4,128)}, s32[4,131072]{1,0:T(4,128)S(1)}, ...), condition=%wide.region_5.6_spmd.clone, body=%wide.region_0.5_spmd.clone.sunk | while | flops 293994496 | bytes 55052548 | solution.py:55
  2.9 1.8 %and_select_fusion.4 = (s32[1,131072]{1,0:T(1,128)S(1)}, s32[1,131072]{1,0:T(1,128)S(1)}) fusion(s32[4,131072]{1,0:T(4,128)S(1)} %get-tuple-element.187, s32[]{:T(128)S(6)} %copy.20), kind=kLoop, calls=%fused_computation.5.clone.1 | loop fusion | flops 1441792 | bytes 1572868 | tf_op jit(solution)/shard_map/while/body/eval_jaxpr/jit(remainder)/select_n | solution.py:25
  4.7 2.2 %and_select_fusion.5 = s32[1,131072]{1,0:T(1,128)S(1)} fusion(s32[1,131072]{1,0:T(1,128)S(1)} %get-tuple-element.164, s32[4,131072]{1,0:T(4,128)S(1)} %get-tuple-element.187, s32[]{:T(128)S(6)} %copy.20), kind=kLoop, calls=%fused_computation.6.clone.1 | loop fusion | flops 1572864 | bytes 1572868 | tf_op jit(solution)/shard_map/while/body/eval_jaxpr/jit(floor_divide)/jit(_where)/select_n | solution.py:26
  8.0 11.0 %select_reduce_fusion.2 = f32[4,131072]{1,0:T(4,128)S(1)} fusion(pred[16,131072]{1,0:T(8,128)(4,1)S(1)} %iota_compare_fusion.4, bf16[64,16]{0,1:T(8,128)(2,1)S(1)} %get-tuple-element.188, s32[131072]{0:T(1024)S(1)} %bitcast.60), kind=kOutput, calls=%fused_computation.clone.1 | convolution fusion | flops 286785536 | bytes 4720640 | tf_op jit(solution)/shard_map/while/body/eval_jaxpr/dot_general | solution.py:30
  21.6 2.9 %slice.46 = f32[3,2,65536]{2,1,0:T(2,128)} reshape(f32[3,131072]{1,0:T(4,128)S(1)} %bitcast.58) | data formatting | bytes 3145728 | tf_op jit(solution)/shard_map/while/body/eval_jaxpr/slice | solution.py:51
  26.3 2.8 %multiply_reduce_fusion.2 = f32[3,65536]{1,0:T(4,128)S(1)} fusion(f32[3,2,65536]{2,1,0:T(2,128)S(1)} %copy-done.1, f32[2,65536]{1,0:T(2,128)S(1)} %exponential_multiply_fusion.2), kind=kLoop, calls=%fused_computation.7.clone.1 | loop fusion | flops 589824 | bytes 2883584 | tf_op jit(solution)/shard_map/while/body/eval_jaxpr/reduce_sum | solution.py:51
  30.7 1.8 %and_select_fusion.4 = (s32[1,131072]{1,0:T(1,128)S(1)}, s32[1,131072]{1,0:T(1,128)S(1)}) fusion(s32[4,131072]{1,0:T(4,128)S(1)} %get-tuple-element.187, s32[]{:T(128)S(6)} %copy.20), kind=kLoop, calls=%fused_computation.5.clone.1 | loop fusion | flops 1441792 | bytes 1572868 | tf_op jit(solution)/shard_map/while/body/eval_jaxpr/jit(remainder)/select_n | solution.py:25
  32.5 2.2 %and_select_fusion.5 = s32[1,131072]{1,0:T(1,128)S(1)} fusion(s32[1,131072]{1,0:T(1,128)S(1)} %get-tuple-element.164, s32[4,131072]{1,0:T(4,128)S(1)} %get-tuple-element.187, s32[]{:T(128)S(6)} %copy.20), kind=kLoop, calls=%fused_computation.6.clone.1 | loop fusion | flops 1572864 | bytes 1572868 | tf_op jit(solution)/shard_map/while/body/eval_jaxpr/jit(floor_divide)/jit(_where)/select_n | solution.py:26
  35.8 11.0 %select_reduce_fusion.2 = f32[4,131072]{1,0:T(4,128)S(1)} fusion(pred[16,131072]{1,0:T(8,128)(4,1)S(1)} %iota_compare_fusion.4, bf16[64,16]{0,1:T(8,128)(2,1)S(1)} %get-tuple-element.188, s32[131072]{0:T(1024)S(1)} %bitcast.60), kind=kOutput, calls=%fused_computation.clone.1 | convolution fusion | flops 286785536 | bytes 4720640 | tf_op jit(solution)/shard_map/while/body/eval_jaxpr/dot_general | solution.py:30
  49.5 2.9 %slice.46 = f32[3,2,65536]{2,1,0:T(2,128)} reshape(f32[3,131072]{1,0:T(4,128)S(1)} %bitcast.58) | data formatting | bytes 3145728 | tf_op jit(solution)/shard_map/while/body/eval_jaxpr/slice | solution.py:51
  54.1 2.8 %multiply_reduce_fusion.2 = f32[3,65536]{1,0:T(4,128)S(1)} fusion(f32[3,2,65536]{2,1,0:T(2,128)S(1)} %copy-done.1, f32[2,65536]{1,0:T(2,128)S(1)} %exponential_multiply_fusion.2), kind=kLoop, calls=%fused_computation.7.clone.1 | loop fusion | flops 589824 | bytes 2883584 | tf_op jit(solution)/shard_map/while/body/eval_jaxpr/reduce_sum | solution.py:51
  60.3 2.2 %and_select_fusion.5 = s32[1,131072]{1,0:T(1,128)S(1)} fusion(s32[1,131072]{1,0:T(1,128)S(1)} %get-tuple-element.164, s32[4,131072]{1,0:T(4,128)S(1)} %get-tuple-element.187, s32[]{:T(128)S(6)} %copy.20), kind=kLoop, calls=%fused_computation.6.clone.1 | loop fusion | flops 1572864 | bytes 1572868 | tf_op jit(solution)/shard_map/while/body/eval_jaxpr/jit(floor_divide)/jit(_where)/select_n | solution.py:26
  63.6 11.0 %select_reduce_fusion.2 = f32[4,131072]{1,0:T(4,128)S(1)} fusion(pred[16,131072]{1,0:T(8,128)(4,1)S(1)} %iota_compare_fusion.4, bf16[64,16]{0,1:T(8,128)(2,1)S(1)} %get-tuple-element.188, s32[131072]{0:T(1024)S(1)} %bitcast.60), kind=kOutput, calls=%fused_computation.clone.1 | convolution fusion | flops 286785536 | bytes 4720640 | tf_op jit(solution)/shard_map/while/body/eval_jaxpr/dot_general | solution.py:30
  77.3 2.9 %slice.46 = f32[3,2,65536]{2,1,0:T(2,128)} reshape(f32[3,131072]{1,0:T(4,128)S(1)} %bitcast.58) | data formatting | bytes 3145728 | tf_op jit(solution)/shard_map/while/body/eval_jaxpr/slice | solution.py:51
  82.0 2.8 %multiply_reduce_fusion.2 = f32[3,65536]{1,0:T(4,128)S(1)} fusion(f32[3,2,65536]{2,1,0:T(2,128)S(1)} %copy-done.1, f32[2,65536]{1,0:T(2,128)S(1)} %exponential_multiply_fusion.2), kind=kLoop, calls=%fused_computation.7.clone.1 | loop fusion | flops 589824 | bytes 2883584 | tf_op jit(solution)/shard_map/while/body/eval_jaxpr/reduce_sum | solution.py:51
  88.2 2.2 %and_select_fusion.5 = s32[1,131072]{1,0:T(1,128)S(1)} fusion(s32[1,131072]{1,0:T(1,128)S(1)} %get-tuple-element.164, s32[4,131072]{1,0:T(4,128)S(1)} %get-tuple-element.187, s32[]{:T(128)S(6)} %copy.20), kind=kLoop, calls=%fused_computation.6.clone.1 | loop fusion | flops 1572864 | bytes 1572868 | tf_op jit(solution)/shard_map/while/body/eval_jaxpr/jit(floor_divide)/jit(_where)/select_n | solution.py:26
  91.5 11.0 %select_reduce_fusion.2 = f32[4,131072]{1,0:T(4,128)S(1)} fusion(pred[16,131072]{1,0:T(8,128)(4,1)S(1)} %iota_compare_fusion.4, bf16[64,16]{0,1:T(8,128)(2,1)S(1)} %get-tuple-element.188, s32[131072]{0:T(1024)S(1)} %bitcast.60), kind=kOutput, calls=%fused_computation.clone.1 | convolution fusion | flops 286785536 | bytes 4720640 | tf_op jit(solution)/shard_map/while/body/eval_jaxpr/dot_general | solution.py:30
  105.1 2.9 %slice.46 = f32[3,2,65536]{2,1,0:T(2,128)} reshape(f32[3,131072]{1,0:T(4,128)S(1)} %bitcast.58) | data formatting | bytes 3145728 | tf_op jit(solution)/shard_map/while/body/eval_jaxpr/slice | solution.py:51
  109.8 2.8 %multiply_reduce_fusion.2 = f32[3,65536]{1,0:T(4,128)S(1)} fusion(f32[3,2,65536]{2,1,0:T(2,128)S(1)} %copy-done.1, f32[2,65536]{1,0:T(2,128)S(1)} %exponential_multiply_fusion.2), kind=kLoop, calls=%fused_computation.7.clone.1 | loop fusion | flops 589824 | bytes 2883584 | tf_op jit(solution)/shard_map/while/body/eval_jaxpr/reduce_sum | solution.py:51
  114.3 2.7 %pad_maximum_fusion = f32[1,4,256,256]{3,1,0,2:T(4,128)} fusion(f32[1,1,256,256]{3,1,0,2:T(1,128)S(1)} %bitcast.69, f32[1,3,256,256]{3,1,0,2:T(4,128)} %bitcast.61), kind=kLoop, calls=%fused_computation.17 | loop fusion | flops 262144 | bytes 2097152 | tf_op jit(solution)/shard_map/concatenate | solution.py:57
  116.9 5.2 %all-to-all-start = ((f32[1,4,256,256]{3,1,0,2:T(4,128)}), f32[1,4,256,256]{3,1,0,2:T(4,128)S(1)}, u32[]{:S(2)}, u32[]{:S(2)}) async-start(f32[1,4,256,256]{3,1,0,2:T(4,128)} %pad_maximum_fusion), calls=%async_computation | async-start | bytes 2097152 | tf_op jit(solution)/shard_map/all_to_all | solution.py:79
  122.4 13.4 %all-to-all-done = f32[1,4,256,256]{3,1,0,2:T(4,128)S(1)} async-done(((f32[1,4,256,256]{3,1,0,2:T(4,128)}), f32[1,4,256,256]{3,1,0,2:T(4,128)S(1)}, u32[]{:S(2)}, u32[]{:S(2)}) %all-to-all-start) | async-done | bytes 1048608 | tf_op jit(solution)/shard_map/all_to_all | solution.py:79
  139.7 2.5 %collective-permute-start.2 = (f32[1,4,8,256]{3,2,0,1:T(8,128)S(1)}, f32[1,4,8,256]{3,2,0,1:T(8,128)S(1)}, u32[]{:S(2)}, u32[]{:S(2)}) collective-permute-start(f32[1,4,8,256]{3,2,0,1:T(8,128)S(1)} %get-tuple-element.126), channel_id=1, source_target_pairs={{0,3},{1,4},{2,5},{3,6},{4,7},{5,0},{6,1},{7,2},{8,11},{9,12},{10,... | collective-permute-start | bytes 98312 | tf_op jit(solution)/shard_map/ppermute | solution.py:90
  (118 shorter events, 43.4 us)
Async XLA Ops:
  0.0 122.1 %copy-start = (s32[8,4]{0,1:T(4,128)S(1)}, s32[8,4]{0,1:T(4,128)}, u32[]{:S(2)}) copy-start(s32[8,4]{0,1:T(4,128)} %param.9) | copy-start | bytes 388
  0.0 2.7 %copy-start.8 = (bf16[256]{0:T(256)(128)(2,1)S(1)}, bf16[256]{0:T(256)(128)(2,1)}, u32[]{:S(2)}) copy-start(bf16[256]{0:T(256)(128)(2,1)} %param.8) | copy-start | bytes 1540
  0.0 2.7 %copy-start.7 = (bf16[3,256]{1,0:T(4,128)(2,1)S(1)}, bf16[3,256]{1,0:T(4,128)(2,1)}, u32[]{:S(2)}) copy-start(bf16[3,256]{1,0:T(4,128)(2,1)} %param.7) | copy-start | bytes 4612
  2.9 5.1 %copy-start.4 = (s32[4,131072]{1,0:T(4,128)}, s32[4,131072]{1,0:T(4,128)S(1)}, u32[]{:S(2)}) copy-start(s32[4,131072]{1,0:T(4,128)S(1)} %get-tuple-element.187) | copy-start | bytes 6291460 | tf_op jit(solution)/shard_map/while
  24.5 1.8 %copy-start.1 = (f32[3,2,65536]{2,1,0:T(2,128)S(1)}, f32[3,2,65536]{2,1,0:T(2,128)}, u32[]{:S(2)}) copy-start(f32[3,2,65536]{2,1,0:T(2,128)} %slice.46) | copy-start | bytes 4718596 | tf_op jit(solution)/shard_map/while
  25.6 3.6 %copy-start.2 = (f32[3,65536]{1,0:T(4,128)S(1)}, f32[3,65536]{1,0:T(4,128)}, u32[]{:S(2)}) copy-start(f32[3,65536]{1,0:T(4,128)} %get-tuple-element.178) | copy-start | bytes 2359300 | tf_op jit(solution)/shard_map/while
  30.7 5.1 %copy-start.4 = (s32[4,131072]{1,0:T(4,128)}, s32[4,131072]{1,0:T(4,128)S(1)}, u32[]{:S(2)}) copy-start(s32[4,131072]{1,0:T(4,128)S(1)} %get-tuple-element.187) | copy-start | bytes 6291460 | tf_op jit(solution)/shard_map/while
  52.3 1.8 %copy-start.1 = (f32[3,2,65536]{2,1,0:T(2,128)S(1)}, f32[3,2,65536]{2,1,0:T(2,128)}, u32[]{:S(2)}) copy-start(f32[3,2,65536]{2,1,0:T(2,128)} %slice.46) | copy-start | bytes 4718596 | tf_op jit(solution)/shard_map/while
  53.4 3.6 %copy-start.2 = (f32[3,65536]{1,0:T(4,128)S(1)}, f32[3,65536]{1,0:T(4,128)}, u32[]{:S(2)}) copy-start(f32[3,65536]{1,0:T(4,128)} %get-tuple-element.178) | copy-start | bytes 2359300 | tf_op jit(solution)/shard_map/while
  58.6 5.1 %copy-start.4 = (s32[4,131072]{1,0:T(4,128)}, s32[4,131072]{1,0:T(4,128)S(1)}, u32[]{:S(2)}) copy-start(s32[4,131072]{1,0:T(4,128)S(1)} %get-tuple-element.187) | copy-start | bytes 6291460 | tf_op jit(solution)/shard_map/while
  80.1 1.8 %copy-start.1 = (f32[3,2,65536]{2,1,0:T(2,128)S(1)}, f32[3,2,65536]{2,1,0:T(2,128)}, u32[]{:S(2)}) copy-start(f32[3,2,65536]{2,1,0:T(2,128)} %slice.46) | copy-start | bytes 4718596 | tf_op jit(solution)/shard_map/while
  81.2 3.6 %copy-start.2 = (f32[3,65536]{1,0:T(4,128)S(1)}, f32[3,65536]{1,0:T(4,128)}, u32[]{:S(2)}) copy-start(f32[3,65536]{1,0:T(4,128)} %get-tuple-element.178) | copy-start | bytes 2359300 | tf_op jit(solution)/shard_map/while
  86.4 5.1 %copy-start.4 = (s32[4,131072]{1,0:T(4,128)}, s32[4,131072]{1,0:T(4,128)S(1)}, u32[]{:S(2)}) copy-start(s32[4,131072]{1,0:T(4,128)S(1)} %get-tuple-element.187) | copy-start | bytes 6291460 | tf_op jit(solution)/shard_map/while
  108.0 1.8 %copy-start.1 = (f32[3,2,65536]{2,1,0:T(2,128)S(1)}, f32[3,2,65536]{2,1,0:T(2,128)}, u32[]{:S(2)}) copy-start(f32[3,2,65536]{2,1,0:T(2,128)} %slice.46) | copy-start | bytes 4718596 | tf_op jit(solution)/shard_map/while
  109.0 3.6 %copy-start.2 = (f32[3,65536]{1,0:T(4,128)S(1)}, f32[3,65536]{1,0:T(4,128)}, u32[]{:S(2)}) copy-start(f32[3,65536]{1,0:T(4,128)} %get-tuple-element.178) | copy-start | bytes 2359300 | tf_op jit(solution)/shard_map/while
  112.6 1.6 %copy-start.5 = (s32[4,131072]{1,0:T(4,128)S(1)}, s32[4,131072]{1,0:T(4,128)}, u32[]{:S(2)}) copy-start(s32[4,131072]{1,0:T(4,128)} %copy-done.4) | copy-start | bytes 6291460 | tf_op jit(solution)/shard_map/while
  116.9 18.8 %all-to-all-start = ((f32[1,4,256,256]{3,1,0,2:T(4,128)}), f32[1,4,256,256]{3,1,0,2:T(4,128)S(1)}, u32[]{:S(2)}, u32[]{:S(2)}) async-start(f32[1,4,256,256]{3,1,0,2:T(4,128)} %pad_maximum_fusion), calls=%async_computation | async-start | bytes 2097152 | tf_op jit(solution)/shard_map/all_to_all | solution.py:79
  138.0 6.7 %collective-permute-start = (f32[1,4,8,256]{3,2,0,1:T(8,128)S(1)}, f32[1,4,8,256]{3,2,0,1:T(8,128)S(1)}, u32[]{:S(2)}, u32[]{:S(2)}) collective-permute-start(f32[1,4,8,256]{3,2,0,1:T(8,128)S(1)} %get-tuple-element.124), channel_id=1, source_target_pairs={{0,1},{1,2},{2,3},{3,4},{4,5},{5,6},{6,7},{7,0},{8,9},{9,10},{10,1... | collective-permute-start | bytes 98312 | tf_op jit(solution)/shard_map/ppermute | solution.py:90
  138.1 8.0 %collective-permute-start.1 = (f32[1,4,8,256]{3,2,0,1:T(8,128)S(1)}, f32[1,4,8,256]{3,2,0,1:T(8,128)S(1)}, u32[]{:S(2)}, u32[]{:S(2)}) collective-permute-start(f32[1,4,8,256]{3,2,0,1:T(8,128)S(1)} %get-tuple-element.125), channel_id=1, source_target_pairs={{0,2},{1,3},{2,4},{3,5},{4,6},{5,7},{6,0},{7,1},{8,10},{9,11},{10,... | collective-permute-start | bytes 98312 | tf_op jit(solution)/shard_map/ppermute | solution.py:90
  139.7 7.8 %collective-permute-start.2 = (f32[1,4,8,256]{3,2,0,1:T(8,128)S(1)}, f32[1,4,8,256]{3,2,0,1:T(8,128)S(1)}, u32[]{:S(2)}, u32[]{:S(2)}) collective-permute-start(f32[1,4,8,256]{3,2,0,1:T(8,128)S(1)} %get-tuple-element.126), channel_id=1, source_target_pairs={{0,3},{1,4},{2,5},{3,6},{4,7},{5,0},{6,1},{7,2},{8,11},{9,12},{10,... | collective-permute-start | bytes 98312 | tf_op jit(solution)/shard_map/ppermute | solution.py:90
  142.3 5.3 %collective-permute-start.3 = (f32[1,4,8,256]{3,2,0,1:T(8,128)S(1)}, f32[1,4,8,256]{3,2,0,1:T(8,128)S(1)}, u32[]{:S(2)}, u32[]{:S(2)}) collective-permute-start(f32[1,4,8,256]{3,2,0,1:T(8,128)S(1)} %get-tuple-element.127), channel_id=1, source_target_pairs={{0,4},{1,5},{2,6},{3,7},{4,0},{5,1},{6,2},{7,3},{8,12},{9,13},{10,... | collective-permute-start | bytes 98312 | tf_op jit(solution)/shard_map/ppermute | solution.py:90
  143.5 4.1 %collective-permute-start.4 = (f32[1,4,8,256]{3,2,0,1:T(8,128)S(1)}, f32[1,4,8,256]{3,2,0,1:T(8,128)S(1)}, u32[]{:S(2)}, u32[]{:S(2)}) collective-permute-start(f32[1,4,8,256]{3,2,0,1:T(8,128)S(1)} %get-tuple-element.128), channel_id=1, source_target_pairs={{0,5},{1,6},{2,7},{3,0},{4,1},{5,2},{6,3},{7,4},{8,13},{9,14},{10,... | collective-permute-start | bytes 98312 | tf_op jit(solution)/shard_map/ppermute | solution.py:90
  144.7 3.9 %collective-permute-start.5 = (f32[1,4,8,256]{3,2,0,1:T(8,128)S(1)}, f32[1,4,8,256]{3,2,0,1:T(8,128)S(1)}, u32[]{:S(2)}, u32[]{:S(2)}) collective-permute-start(f32[1,4,8,256]{3,2,0,1:T(8,128)S(1)} %fusion.20), channel_id=1, source_target_pairs={{0,6},{1,7},{2,0},{3,1},{4,2},{5,3},{6,4},{7,5},{8,14},{9,15},{10,... | collective-permute-start | bytes 98312 | tf_op jit(solution)/shard_map/ppermute | solution.py:90
  146.0 3.0 %collective-permute-start.6 = (f32[1,4,8,256]{3,2,0,1:T(8,128)S(1)}, f32[1,4,8,256]{3,2,0,1:T(8,128)S(1)}, u32[]{:S(2)}, u32[]{:S(2)}) collective-permute-start(f32[1,4,8,256]{3,2,0,1:T(8,128)S(1)} %get-tuple-element.123), channel_id=1, source_target_pairs={{0,7},{1,0},{2,1},{3,2},{4,3},{5,4},{6,5},{7,6},{8,15},{9,8},{10,9... | collective-permute-start | bytes 98312 | tf_op jit(solution)/shard_map/ppermute | solution.py:90
  (8 other events, 9.4 us)
